TPU v7x, 32 devices: a whole 2x2x4 slice. The times are simulated.
32 devices in a mesh: exp: 8 (over y, x, core), tp: 4 (over z).
Axes of the slice: x: 2, y: 2, z: 4, core: 2. Of those that a mesh axis runs over, the one named last changes fastest.
Arguments:
- tokens: bfloat16 [224, 4096], P('exp', 'tp'), may hold values from -6 to 6
- cotangent: bfloat16 [224, 4096], P('exp', 'tp'), may hold values from -6 to 6
- experts: int32 [224, 2], P('exp'), may hold values from 0 to 7, all different within a row; in each aligned block of 28 rows (0 to 27, 28 to 55, ...) at most 8 rows name the same one
- gates: float32 [224, 2], P('exp'), may hold values from 0.1 to 0.9
- w_gate: bfloat16 [8, 4096, 8192], P('exp', None, 'tp'), may hold values from -0.09375 to 0.09375
- w_up: bfloat16 [8, 4096, 8192], P('exp', None, 'tp'), may hold values from -0.09375 to 0.09375
- w_down: bfloat16 [8, 8192, 4096], P('exp', 'tp'), may hold values from -0.0625 to 0.0625
Outputs:
- output: bfloat16 [224, 4096], P('exp', 'tp')
- input_grad: bfloat16 [224, 4096], P('exp', 'tp')
- grad_gate: bfloat16 [8, 4096, 8192], P('exp', None, 'tp')
- grad_up: bfloat16 [8, 4096, 8192], P('exp', None, 'tp')
- grad_down: bfloat16 [8, 8192, 4096], P('exp', 'tp')
Inputs may be any that keep to these rules, and one draw needn't show every extreme that they name: Each row names 2 different experts. In each aligned block of 28 rows (the rows of one index of exp) no expert is named by more than 8 rows, and in some blocks one is named by exactly 8.
All inputs are finite; a program needn't handle non-finite values.
Results may differ from a plain program's by a relative error of at most 0.017.
Values may be sent and summed in bfloat16 or wider, within the bound.
A program may use at most 192 MiB of HBM per device.

v0:
```python
import jax
import jax.numpy as jnp
from jax import lax
from jax.sharding import PartitionSpec as P

EXPERTS = 8
CAP = 8


def contract_rows(left, right):
    return lax.dot_general(
        left, right, (((0,), (0,)), ((), ())), preferred_element_type=jnp.float32
    )


def contract_cols(left, right):
    return lax.dot_general(
        left, right, (((1,), (1,)), ((), ())), preferred_element_type=jnp.float32
    )


def slot_places(experts, capacity):
    pair_ids = experts.reshape(-1)
    matches = (pair_ids[:, None] == jnp.arange(EXPERTS, dtype=jnp.int32)[None, :]).astype(jnp.int32)
    before = jnp.cumsum(matches, axis=0) - matches
    slot_ids = jnp.sum(before * matches, axis=1)
    return pair_ids * capacity + slot_ids


def per_device(tokens, cotangent, experts, gates, w_gate, w_up, w_down):
    exp_devices = lax.axis_size("exp")
    group_size = exp_devices // EXPERTS
    capacity = CAP
    tok_rows, top_count = experts.shape
    model_width = w_gate.shape[1]
    gate_mat = w_gate[0]
    up_mat = w_up[0]
    down_mat = w_down[0]
    row_count = exp_devices * capacity
    places = slot_places(experts, capacity)
    pick_table = (
        places[:, None] == jnp.arange(EXPERTS * capacity, dtype=jnp.int32)[None, :]
    ).astype(jnp.float32)
    per_token = pick_table.reshape(tok_rows, top_count, EXPERTS * capacity)
    weighted = jnp.sum(per_token * gates[:, :, None], axis=1)
    unweighted = jnp.sum(per_token, axis=1)
    pick_low = pick_table.astype(jnp.bfloat16)
    scaled = (gates[:, :, None] * cotangent[:, None, :].astype(jnp.float32)).astype(jnp.bfloat16)
    scaled = scaled.reshape(tok_rows * top_count, cotangent.shape[1])

    def merge_group(received):
        col_count = received.shape[2]
        summed = jnp.sum(received.reshape(EXPERTS, group_size, capacity, col_count), axis=1)
        return summed.reshape(EXPERTS * capacity, col_count)

    def gather_tokens(table, received):
        return jnp.dot(
            table,
            merge_group(received),
            precision=lax.Precision.HIGHEST,
            preferred_element_type=jnp.float32,
        )

    whole_tokens, whole_scaled = (
        lax.all_gather(tokens, "tp", axis=1, tiled=True),
        lax.all_gather(scaled, "tp", axis=1, tiled=True),
    )
    col_count = whole_tokens.shape[1]
    repeated = jnp.repeat(whole_tokens, top_count, axis=0)
    token_send = contract_rows(pick_low, repeated).astype(jnp.bfloat16)
    grad_send = contract_rows(pick_low, whole_scaled).astype(jnp.bfloat16)
    token_send = jnp.broadcast_to(
        token_send.reshape(EXPERTS, 1, capacity, col_count),
        (EXPERTS, group_size, capacity, col_count),
    )
    grad_send = jnp.broadcast_to(
        grad_send.reshape(EXPERTS, 1, capacity, col_count),
        (EXPERTS, group_size, capacity, col_count),
    )
    token_send, grad_send = (
        token_send.reshape(exp_devices, capacity, col_count),
        grad_send.reshape(exp_devices, capacity, col_count),
    )
    token_rows, cot_rows = (
        lax.all_to_all(token_send, "exp", split_axis=0, concat_axis=0, tiled=True),
        lax.all_to_all(grad_send, "exp", split_axis=0, concat_axis=0, tiled=True),
    )
    token_rows = token_rows.reshape(row_count, model_width)
    cot_rows = cot_rows.reshape(row_count, model_width)
    hidden_gate = jnp.dot(token_rows, gate_mat, preferred_element_type=jnp.float32)
    hidden_up = jnp.dot(token_rows, up_mat, preferred_element_type=jnp.float32)
    grad_act = contract_cols(cot_rows, down_mat)
    sigmoid_gate = jax.nn.sigmoid(hidden_gate)
    activation = (hidden_gate * sigmoid_gate * hidden_up).astype(jnp.bfloat16)
    out_term = jnp.dot(activation, down_mat, preferred_element_type=jnp.float32)
    grad_first = (
        grad_act * hidden_up * sigmoid_gate * (1.0 + hidden_gate * (1.0 - sigmoid_gate))
    ).astype(jnp.bfloat16)
    grad_second = (grad_act * hidden_gate * sigmoid_gate).astype(jnp.bfloat16)
    grad_down = contract_rows(activation, cot_rows).astype(jnp.bfloat16)
    grad_gate = contract_rows(token_rows, grad_first).astype(jnp.bfloat16)
    grad_up = contract_rows(token_rows, grad_second).astype(jnp.bfloat16)
    back_term = contract_cols(grad_first, gate_mat) + contract_cols(grad_second, up_mat)
    out_back, grad_back = (
        lax.all_to_all(
            out_term.reshape(exp_devices, capacity, model_width),
            "exp",
            split_axis=0,
            concat_axis=0,
            tiled=True,
        ),
        lax.all_to_all(
            back_term.reshape(exp_devices, capacity, model_width),
            "exp",
            split_axis=0,
            concat_axis=0,
            tiled=True,
        ),
    )
    out_tokens = gather_tokens(weighted, out_back)
    grad_tokens = gather_tokens(unweighted, grad_back)
    output, input_grad = (
        lax.psum_scatter(
            out_tokens.astype(jnp.bfloat16), "tp", scatter_dimension=1, tiled=True
        ).astype(jnp.float32),
        lax.psum_scatter(
            grad_tokens.astype(jnp.bfloat16), "tp", scatter_dimension=1, tiled=True
        ).astype(jnp.float32),
    )
    return (
        output.astype(jnp.bfloat16),
        input_grad.astype(jnp.bfloat16),
        grad_gate[None],
        grad_up[None],
        grad_down[None],
    )


def solution(mesh):
    in_specs = (
        P("exp", "tp"),
        P("exp", "tp"),
        P("exp", None),
        P("exp", None),
        P("exp", None, "tp"),
        P("exp", None, "tp"),
        P("exp", "tp", None),
    )
    out_specs = (
        P("exp", "tp"),
        P("exp", "tp"),
        P("exp", None, "tp"),
        P("exp", None, "tp"),
        P("exp", "tp", None),
    )
    return jax.shard_map(
        per_device, mesh=mesh, in_specs=in_specs, out_specs=out_specs, check_vma=False
    )
```

profile of v0, /device:TPU:0, one launch (start us, length us, event | category | flops | bytes accessed | tf_op | source)
XLA Modules:
  0.0 172.2 jit_solution(9109463998063205250)
XLA Ops:
  7.2 0.8 copy.30
  7.9 0.1 mul.77
  8.0 0.8 copy.27
  8.8 0.1 eq.35
  8.9 0.1 fusion.29
  9.0 0.1 reduce_window_sum.11
  9.1 0.2 select_reduce_fusion.1
  9.3 0.9 mul.79
  10.2 0.2 mul.80
  10.3 0.1 multiply_convert_fusion.3
  10.4 16.8 %all_gather.7 = bf16[56,4096]{1,0:T(8,128)(2,1)S(1)} all-gather(bf16[56,1024]{1,0:T(8,128)(2,1)S(1)} %multiply_convert_fusion.3), channel_id=1, replica_groups=mesh['exp'=8,'tp'=4] {'tp'}, dimensions={1}, use_global_device_ids=true | all-gather | bytes 573440 | tf_op jit(solution)/shard_map/all_gather | solution.py:66
  27.2 1.2 fusion.19
  28.4 3.7 %all-to-all-start.2 = ((bf16[8,8,4096]{2,1,0:T(8,128)(2,1)}), bf16[8,8,4096]{2,1,0:T(8,128)(2,1)S(1)}, u32[]{:S(2)}, u32[]{:S(2)}) async-start(bf16[8,8,4096]{2,1,0:T(8,128)(2,1)} %fusion.19), calls=%async_computation.3 | async-start | bytes 1048576 | tf_op jit(solution)/shard_map/all_to_all | solution.py:86
  32.1 0.1 reduce_sum.30
  32.2 0.1 copy.28
  32.3 14.9 %all_gather.6 = bf16[28,4096]{1,0:T(8,128)(2,1)S(1)} all-gather(bf16[28,1024]{1,0:T(8,128)(2,1)} %param.7), channel_id=1, replica_groups=mesh['exp'=8,'tp'=4] {'tp'}, dimensions={1}, use_global_device_ids=true | all-gather | bytes 286720 | tf_op jit(solution)/shard_map/all_gather | solution.py:65
  47.2 0.4 broadcast_in_dim.8
  47.6 0.2 reshape.64
  47.8 1.2 fusion.18
  49.0 0.0 all-to-all-done.2
  49.0 3.9 %all-to-all-start = ((bf16[8,8,4096]{2,1,0:T(8,128)(2,1)}), bf16[8,8,4096]{2,1,0:T(8,128)(2,1)S(1)}, u32[]{:S(2)}, u32[]{:S(2)}) async-start(bf16[8,8,4096]{2,1,0:T(8,128)(2,1)} %fusion.18), calls=%async_computation | async-start | bytes 1048576 | tf_op jit(solution)/shard_map/all_to_all | solution.py:85
  52.9 11.0 %fusion.2 = f32[64,2048]{1,0:T(8,128)S(1)} fusion(bf16[1,2048,4096]{2,1,0:T(8,128)(2,1)} %param.13, bf16[8,8,4096]{2,1,0:T(8,128)(2,1)S(1)} %all-to-all-done.2), kind=kOutput, calls=%fused_computation.2 | convolution fusion | flops 1073741824 | bytes 17825792 | tf_op jit(solution)/shard_map/dot_general | solution.py:17
  63.9 0.0 all-to-all-done
  63.9 0.0 slice-start
  63.9 0.0 slice-start.1
  63.9 8.9 %fusion.6 = f32[64,2048]{1,0:T(8,128)S(1)} fusion(bf16[1,4096,2048]{2,1,0:T(8,128)(2,1)} %param.12, bf16[8,8,4096]{2,1,0:T(8,128)(2,1)S(1)} %all-to-all-done), kind=kOutput, calls=%fused_computation.6 | convolution fusion | flops 1073741824 | bytes 17825792 | tf_op jit(solution)/shard_map/dot_general | solution.py:91
  72.9 0.0 slice-start.2
  72.9 0.0 slice-start.3
  72.9 10.0 %multiply_convert_fusion.1 = (bf16[64,2048]{1,0:T(8,128)(2,1)}, bf16[64,2048]{1,0:T(8,128)(2,1)S(1)}, bf16[64,2048]{1,0:T(8,128)(2,1)}) fusion(f32[64,2048]{1,0:T(8,128)S(1)} %fusion.2, f32[64,2048]{1,0:T(8,128)S(1)} %fusion.6, bf16[1,4096,2048]{2,1,0:T(8,128)(2,1)} %param.11, bf16[8,8,4096]{2,1,0:T(8,128)(2,1)S(1)} %all-to-all-done), kind=kOutput, calls=%fused_computation.32 | convolution fusion | flops 1075838976 | bytes 19136512 | tf_op jit(solution)/shard_map/dot_general | solution.py:90
  82.9 4.0 %fusion = f32[8,8,4096]{2,1,0:T(8,128)} fusion(bf16[1,2048,4096]{2,1,0:T(8,128)(2,1)S(1)} %bitcast.69, bf16[64,2048]{1,0:T(8,128)(2,1)S(1)} %get-tuple-element.8), kind=kOutput, calls=%fused_computation | convolution fusion | flops 1073741824 | bytes 18087936 | tf_op jit(solution)/shard_map/dot_general | solution.py:95
  86.9 4.2 %all-to-all-start.1 = ((f32[8,8,4096]{2,1,0:T(8,128)}), f32[8,8,4096]{2,1,0:T(8,128)S(1)}, u32[]{:S(2)}, u32[]{:S(2)}) async-start(f32[8,8,4096]{2,1,0:T(8,128)} %fusion), calls=%async_computation.1 | async-start | bytes 2097152 | tf_op jit(solution)/shard_map/all_to_all | solution.py:105
  91.1 11.0 %fusion.4 = f32[64,4096]{1,0:T(8,128)S(1)} fusion(bf16[64,2048]{1,0:T(8,128)(2,1)} %get-tuple-element.9, bf16[1,4096,2048]{2,1,0:T(8,128)(2,1)} %param.12), kind=kOutput, calls=%fused_computation.4 | convolution fusion | flops 1073741824 | bytes 18087936 | tf_op jit(solution)/shard_map/dot_general | solution.py:17
  102.2 12.0 %fusion.15 = f32[8,8,4096]{2,1,0:T(8,128)} fusion(f32[64,4096]{1,0:T(8,128)S(1)} %fusion.4, bf16[64,2048]{1,0:T(8,128)(2,1)} %get-tuple-element.7, bf16[1,4096,2048]{2,1,0:T(8,128)(2,1)} %param.11), kind=kOutput, calls=%fused_computation.16 | convolution fusion | flops 1074003968 | bytes 19136512 | tf_op jit(solution)/shard_map/dot_general | solution.py:17
  114.2 0.0 all-to-all-done.1
  114.2 4.2 %all-to-all-start.3 = ((f32[8,8,4096]{2,1,0:T(8,128)}), f32[8,8,4096]{2,1,0:T(8,128)S(1)}, u32[]{:S(2)}, u32[]{:S(2)}) async-start(f32[8,8,4096]{2,1,0:T(8,128)} %fusion.15), calls=%async_computation.4 | async-start | bytes 2097152 | tf_op jit(solution)/shard_map/all_to_all | solution.py:112
  118.4 0.0 reduce-scatter.3.cloned.1.call-start
  118.5 0.1 copy.29
  118.6 0.1 convert_reduce_fusion
  118.7 1.3 convolution_convert_fusion.3
  120.1 0.0 reduce-scatter.3.cloned.1.call-update
  120.1 0.3 reduce-scatter.5.cloned.1.call-start
  120.4 9.5 %convert_bitcast_fusion.2 = bf16[1,4096,2048]{2,1,0:T(8,128)(2,1)} fusion(bf16[64,2048]{1,0:T(8,128)(2,1)} %get-tuple-element.7, bf16[8,8,4096]{2,1,0:T(8,128)(2,1)S(1)} %all-to-all-done), kind=kOutput, calls=%fused_computation.14 | convolution fusion | flops 1082130432 | bytes 17563648 | tf_op jit(solution)/shard_map/dot_general | solution.py:11
  129.9 3.9 %all-to-all-done.3 = f32[8,8,4096]{2,1,0:T(8,128)S(1)} async-done(((f32[8,8,4096]{2,1,0:T(8,128)}), f32[8,8,4096]{2,1,0:T(8,128)S(1)}, u32[]{:S(2)}, u32[]{:S(2)}) %all-to-all-start.3) | async-done | bytes 1048608 | tf_op jit(solution)/shard_map/all_to_all | solution.py:112
  133.8 1.3 convolution_convert_fusion.2
  135.1 0.0 reduce-scatter.5.cloned.1.call-update
  135.1 8.5 %convert_bitcast_fusion.1 = bf16[1,4096,2048]{2,1,0:T(8,128)(2,1)} fusion(bf16[64,2048]{1,0:T(8,128)(2,1)S(1)} %copy-done, bf16[8,8,4096]{2,1,0:T(8,128)(2,1)S(1)} %all-to-all-done), kind=kOutput, calls=%fused_computation.13 | convolution fusion | flops 1082130432 | bytes 17563648 | tf_op jit(solution)/shard_map/dot_general | solution.py:11
  143.7 8.5 %convert_bitcast_fusion = bf16[1,2048,4096]{2,1,0:T(8,128)(2,1)} fusion(bf16[64,2048]{1,0:T(8,128)(2,1)S(1)} %get-tuple-element.8, bf16[8,8,4096]{2,1,0:T(8,128)(2,1)S(1)} %all-to-all-done.2), kind=kOutput, calls=%fused_computation.12 | convolution fusion | flops 1082130432 | bytes 17563648 | tf_op jit(solution)/shard_map/dot_general | solution.py:11
  152.2 13.1 %reduce-scatter.5.cloned.1.call-done = bf16[28,1024]{1,0:T(8,128)(2,1)} async-done(((bf16[28,4096]{1,0:T(8,128)(2,1)}), bf16[28,1024]{1,0:T(8,128)(2,1)}) %reduce-scatter.5.cloned.1.call-update) | async-done | bytes 57360 | tf_op jit(solution)/shard_map/reduce_scatter | solution.py:126
  (12 shorter events, 0.0 us)
Async XLA Ops:
  28.4 20.6 %all-to-all-start.2 = ((bf16[8,8,4096]{2,1,0:T(8,128)(2,1)}), bf16[8,8,4096]{2,1,0:T(8,128)(2,1)S(1)}, u32[]{:S(2)}, u32[]{:S(2)}) async-start(bf16[8,8,4096]{2,1,0:T(8,128)(2,1)} %fusion.19), calls=%async_computation.3 | async-start | bytes 1048576 | tf_op jit(solution)/shard_map/all_to_all | solution.py:86
  49.0 14.9 %all-to-all-start = ((bf16[8,8,4096]{2,1,0:T(8,128)(2,1)}), bf16[8,8,4096]{2,1,0:T(8,128)(2,1)S(1)}, u32[]{:S(2)}, u32[]{:S(2)}) async-start(bf16[8,8,4096]{2,1,0:T(8,128)(2,1)} %fusion.18), calls=%async_computation | async-start | bytes 1048576 | tf_op jit(solution)/shard_map/all_to_all | solution.py:85
  63.9 18.9 %slice-start = ((s8[16777216]{0:T(1024)(128)(4,1)}), s8[4194304]{0:T(1024)(128)(4,1)S(1)}, s32[]{:S(2)}) async-start(s8[16777216]{0:T(1024)(128)(4,1)} %bitcast.68), calls=%async_computation.8 | async-start | bytes 8388608
  63.9 18.9 %slice-start.1 = ((s8[16777216]{0:T(1024)(128)(4,1)}), s8[4194304]{0:T(1024)(128)(4,1)S(1)}, s32[]{:S(2)}) async-start(s8[16777216]{0:T(1024)(128)(4,1)} %bitcast.68), calls=%async_computation.9 | async-start | bytes 8388608
  72.9 10.0 %slice-start.2 = ((s8[16777216]{0:T(1024)(128)(4,1)}), s8[4194304]{0:T(1024)(128)(4,1)S(1)}, s32[]{:S(2)}) async-start(s8[16777216]{0:T(1024)(128)(4,1)} %bitcast.68), calls=%async_computation.10 | async-start | bytes 8388608
  72.9 10.0 %slice-start.3 = ((s8[16777216]{0:T(1024)(128)(4,1)}), s8[4194304]{0:T(1024)(128)(4,1)S(1)}, s32[]{:S(2)}) async-start(s8[16777216]{0:T(1024)(128)(4,1)} %bitcast.68), calls=%async_computation.11 | async-start | bytes 8388608
  86.9 27.3 %all-to-all-start.1 = ((f32[8,8,4096]{2,1,0:T(8,128)}), f32[8,8,4096]{2,1,0:T(8,128)S(1)}, u32[]{:S(2)}, u32[]{:S(2)}) async-start(f32[8,8,4096]{2,1,0:T(8,128)} %fusion), calls=%async_computation.1 | async-start | bytes 2097152 | tf_op jit(solution)/shard_map/all_to_all | solution.py:105
  91.1 27.3 %copy-start.1 = (s32[28,2]{0,1:T(2,128)S(1)}, s32[28,2]{0,1:T(2,128)}, u32[]{:S(2)}) copy-start(s32[28,2]{0,1:T(2,128)} %param.9) | copy-start | bytes 676
  114.2 19.6 %all-to-all-start.3 = ((f32[8,8,4096]{2,1,0:T(8,128)}), f32[8,8,4096]{2,1,0:T(8,128)S(1)}, u32[]{:S(2)}, u32[]{:S(2)}) async-start(f32[8,8,4096]{2,1,0:T(8,128)} %fusion.15), calls=%async_computation.4 | async-start | bytes 2097152 | tf_op jit(solution)/shard_map/all_to_all | solution.py:112
  118.4 33.8 %reduce-scatter.3.cloned.1.call-start = ((), (), s32[]{:S(2)}) async-start(), calls=%async_computation.6 | async-start | bytes 327680 | tf_op jit(solution)/shard_map/reduce_scatter | solution.py:123
  120.1 15.1 %copy-start = (bf16[64,2048]{1,0:T(8,128)(2,1)S(1)}, bf16[64,2048]{1,0:T(8,128)(2,1)}, u32[]{:S(2)}) copy-start(bf16[64,2048]{1,0:T(8,128)(2,1)} %get-tuple-element.9) | copy-start | bytes 786436
  120.1 45.3 %reduce-scatter.5.cloned.1.call-start = ((), (), s32[]{:S(2)}) async-start(), calls=%async_computation.7 | async-start | bytes 327680 | tf_op jit(solution)/shard_map/reduce_scatter | solution.py:126
Sparse Core Ops, SparseCore 0:
  122.0 22.2 reduce-scatter.2
  147.1 18.1 reduce-scatter.4
where the time goes:
time: 173 us; the launch traced here: 172 us
  matrix products  88.6 us (51%)
  blocking collectives  31.7 us (18%)
  waiting for transfers between devices  17 us (10%)
  starting transfers between devices  16.4 us (9%)
  between operations  14.2 us (8%)
  local copies, waits for them, and re-layouts  3.7 us (2%)
    dot_general x3, matrix products, contract_cols(): lax.dot_general(left, right, (((1,), (1,)), ((), ())), preferred_element_...  34 us
    dot_general x5, matrix products, contract_rows(): lax.dot_general(left, right, (((0,), (0,)), ((), ())), preferred_element_...  29 us
    all_gather x1, blocking collectives, per_device(): lax.all_gather(scaled, 'tp', axis=1, tiled=True)  16.8 us
    all_gather x1, blocking collectives, per_device(): lax.all_gather(tokens, 'tp', axis=1, tiled=True)  14.9 us
    reduce_scatter x1, waiting for transfers between devices, per_device(): lax.psum_scatter(grad_tokens.astype(jnp.bfloat16), 'tp', scatter_dimensio...  13.1 us
    dot_general x1, matrix products, per_device(): jnp.dot(token_rows, gate_mat, preferred_element_type=jnp.float32)  9.95 us
    dot_general x1, matrix products, per_device(): hidden_up = jnp.dot(token_rows, up_mat, preferred_element_type=jnp.float32)  8.94 us
    all_to_all x1, starting transfers between devices, per_device(): lax.all_to_all(out_term.reshape(exp_devices, capacity, model_width), 'exp...  4.21 us
  transfers between devices with their start and end apart: 6, of which 2 were waited for; matrix products, arithmetic and copies ran while one was open for 38% of the time, Pallas kernels for 0%

commit v1 on v0

v1 whole, which is shorter than its diff:
```python
import functools

import jax
import jax.numpy as jnp
from jax import lax
from jax.experimental import pallas as pl
from jax.experimental.pallas import tpu as pltpu
from jax.sharding import PartitionSpec as P

EXPERTS = 8
CAP = 8
MESH = pl.DeviceIdType.MESH


def contract_rows(left, right):
    return lax.dot_general(
        left, right, (((0,), (0,)), ((), ())), preferred_element_type=jnp.float32
    )


def contract_cols(left, right):
    return lax.dot_general(
        left, right, (((1,), (1,)), ((), ())), preferred_element_type=jnp.float32
    )


def slot_places(experts, capacity):
    pair_ids = experts.reshape(-1)
    matches = (pair_ids[:, None] == jnp.arange(EXPERTS, dtype=jnp.int32)[None, :]).astype(jnp.int32)
    before = jnp.cumsum(matches, axis=0) - matches
    slot_ids = jnp.sum(before * matches, axis=1)
    return pair_ids * capacity + slot_ids


def forward_kernel(n, m, group, bf, depth, send_ref, wg_hbm, wu_hbm, wd_hbm, *rest):
    x_ref, g_ref, a_ref, d1_ref, d3_ref = rest[:5]
    parts = rest[5 : 5 + m]
    (wg, wu, wd, w_sem, held, y_acc, b_acc, s1, r1, s2, r2) = rest[5 + m :]
    e, t = lax.axis_index("exp"), lax.axis_index("tp")
    cols = send_ref.shape[2]
    blocks = wg_hbm.shape[2] // bf

    def weight_copies(j, slot):
        span = pl.ds(pl.multiple_of(j * bf, bf), bf)
        return (
            pltpu.make_async_copy(wg_hbm.at[0, :, span], wg.at[slot], w_sem.at[slot, 0]),
            pltpu.make_async_copy(wu_hbm.at[0, :, span], wu.at[slot], w_sem.at[slot, 1]),
            pltpu.make_async_copy(wd_hbm.at[0, span, :], wd.at[slot], w_sem.at[slot, 2]),
        )

    barrier = pltpu.get_barrier_semaphore()
    for r in range(1, n):
        pl.semaphore_signal(
            barrier, inc=1, device_id={"exp": lax.rem(e + r, n), "tp": t}, device_id_type=MESH
        )
    for q in range(1, m):
        pl.semaphore_signal(
            barrier, inc=1, device_id={"exp": e, "tp": lax.rem(t + q, m)}, device_id_type=MESH
        )
    for j in range(depth):
        for copy in weight_copies(j, j):
            copy.start()
    pl.semaphore_wait(barrier, n - 1 + m - 1)

    def rows_of(source):
        return pl.ds(pl.multiple_of(source * 2 * CAP, 2 * CAP), 2 * CAP)

    def cols_of(part):
        return pl.ds(pl.multiple_of(part * cols, cols), cols)

    first = []
    for r in range(1, n):
        dest = lax.rem(e + r, n)
        copy = pltpu.make_async_remote_copy(
            src_ref=send_ref.at[dest // group],
            dst_ref=held.at[rows_of(e), cols_of(t)],
            send_sem=s1.at[r],
            recv_sem=r1.at[r],
            device_id={"exp": dest, "tp": t},
            device_id_type=MESH,
        )
        copy.start()
        first.append(copy)
    second = []
    for r in range(n):
        source = lax.rem(e - r + n, n)
        here = held.at[rows_of(source), cols_of(t)]
        if r > 0:
            first[r - 1].wait_recv()
        for q in range(1, m):
            copy = pltpu.make_async_remote_copy(
                src_ref=here if r > 0 else send_ref.at[e // group],
                dst_ref=here,
                send_sem=s2.at[r, q],
                recv_sem=r2.at[r, q],
                device_id={"exp": e, "tp": lax.rem(t + q, m)},
                device_id_type=MESH,
            )
            copy.start()
            second.append(copy)
    held[rows_of(e), cols_of(t)] = send_ref[e // group]
    y_acc[...] = jnp.zeros_like(y_acc)
    b_acc[...] = jnp.zeros_like(b_acc)
    for copy in second:
        copy.wait_recv()
    for part in range(m):
        span = pl.ds(part * cols, cols)
        pair = held[:, span].astype(jnp.float32).reshape(n, 2, CAP, cols)
        x_ref[:, span] = pair[:, 0].reshape(n * CAP, cols).astype(jnp.bfloat16)
        g_ref[:, span] = pair[:, 1].reshape(n * CAP, cols).astype(jnp.bfloat16)

    @pl.loop(0, blocks)
    def _(j):
        slot = lax.rem(j, depth)
        for copy in weight_copies(j, slot):
            copy.wait()
        span = pl.ds(pl.multiple_of(j * bf, bf), bf)
        h1 = jnp.dot(x_ref[...], wg[slot], preferred_element_type=jnp.float32)
        h3 = jnp.dot(x_ref[...], wu[slot], preferred_element_type=jnp.float32)
        da = contract_cols(g_ref[...], wd[slot])
        sig = jax.nn.sigmoid(h1)
        act = (h1 * sig * h3).astype(jnp.bfloat16)
        d1 = (da * h3 * sig * (1.0 + h1 * (1.0 - sig))).astype(jnp.bfloat16)
        d3 = (da * h1 * sig).astype(jnp.bfloat16)
        a_ref[:, span] = act
        d1_ref[:, span] = d1
        d3_ref[:, span] = d3
        y_acc[...] += jnp.dot(act, wd[slot], preferred_element_type=jnp.float32)
        b_acc[...] += contract_cols(d1, wg[slot]) + contract_cols(d3, wu[slot])

        @pl.when(j + depth < blocks)
        def _():
            for copy in weight_copies(j + depth, slot):
                copy.start()

    for r in range(m):
        span = cols_of(lax.rem(t + r, m))
        parts[r][0] = y_acc[:, span].astype(jnp.bfloat16)
        parts[r][1] = b_acc[:, span].astype(jnp.bfloat16)
    for copy in first + second:
        copy.wait_send()


def wide_kernel(x_ref, d1_ref, d3_ref, gate_ref, up_ref, xt):
    @pl.when(pl.program_id(0) == 0)
    def _():
        xt[...] = x_ref[...].astype(jnp.float32).T.astype(jnp.bfloat16)

    gate_ref[0] = jnp.dot(xt[...], d1_ref[...], preferred_element_type=jnp.float32).astype(
        jnp.bfloat16
    )
    up_ref[0] = jnp.dot(xt[...], d3_ref[...], preferred_element_type=jnp.float32).astype(
        jnp.bfloat16
    )


def sum_kernel(_, *rest):
    parts, out_ref = rest[:-1], rest[-1]
    total = parts[0][...].astype(jnp.float32)
    for part in parts[1:]:
        total = total + part[...].astype(jnp.float32)
    n, _, cap, cols = out_ref.shape
    for which in range(2):
        out_ref[:, which] = total[which].reshape(n, cap, cols).astype(out_ref.dtype)


def down_kernel(_, a_ref, g_ref, down_ref):
    down_ref[0] = contract_rows(a_ref[...], g_ref[...]).astype(jnp.bfloat16)


def per_device(tokens, cotangent, experts, gates, w_gate, w_up, w_down):
    n, m = lax.axis_size("exp"), lax.axis_size("tp")
    group = n // EXPERTS
    tok_rows, top_count = experts.shape
    width, hidden = w_gate.shape[1], w_gate.shape[2]
    cols = tokens.shape[1]
    rows = n * CAP
    bf = min(256, hidden)
    blocks = hidden // bf
    depth = min(6, blocks)

    places = slot_places(experts, CAP)
    pick = (
        places[:, None] == jnp.arange(EXPERTS * CAP, dtype=jnp.int32)[None, :]
    ).astype(jnp.float32)
    per_token = pick.reshape(tok_rows, top_count, EXPERTS * CAP)
    weighted = jnp.sum(per_token * gates[:, :, None], axis=1)
    unweighted = jnp.sum(per_token, axis=1)
    row_gate = jnp.sum(weighted, axis=0)
    pick_low = unweighted.astype(jnp.bfloat16)
    both = jnp.concatenate([tokens, cotangent], axis=1)
    picked = contract_rows(pick_low, both)
    token_rows = picked[:, :cols].astype(jnp.bfloat16)
    scaled = (picked[:, cols:] * row_gate[:, None]).astype(jnp.bfloat16)
    send = jnp.concatenate(
        [token_rows.reshape(EXPERTS, CAP, cols), scaled.reshape(EXPERTS, CAP, cols)], axis=1
    )

    vmem = pl.BlockSpec(memory_space=pltpu.VMEM)
    anyw = pl.BlockSpec(memory_space=pl.ANY)
    low = jnp.bfloat16
    wide = jax.ShapeDtypeStruct((rows, width), low)
    narrow = jax.ShapeDtypeStruct((rows, hidden), low)
    part = jax.ShapeDtypeStruct((2, rows, cols), low)
    outs = pl.pallas_call(
        functools.partial(forward_kernel, n, m, group, bf, depth),
        out_shape=[wide, wide, narrow, narrow, narrow] + [part] * m,
        in_specs=[vmem, anyw, anyw, anyw],
        out_specs=[vmem] * (5 + m),
        scratch_shapes=[
            pltpu.VMEM((depth, width, bf), low),
            pltpu.VMEM((depth, width, bf), low),
            pltpu.VMEM((depth, bf, width), low),
            pltpu.SemaphoreType.DMA((depth, 3)),
            pltpu.VMEM((2 * rows, width), low),
            pltpu.VMEM((rows, width), jnp.float32),
            pltpu.VMEM((rows, width), jnp.float32),
            pltpu.SemaphoreType.DMA((n,)),
            pltpu.SemaphoreType.DMA((n,)),
            pltpu.SemaphoreType.DMA((n, m)),
            pltpu.SemaphoreType.DMA((n, m)),
        ],
        compiler_params=pltpu.CompilerParams(
            collective_id=0, has_side_effects=True, vmem_limit_bytes=60 * 1024 * 1024
        ),
        cost_estimate=pl.CostEstimate(
            flops=12 * rows * width * hidden,
            bytes_accessed=6 * width * hidden,
            transcendentals=rows * hidden,
        ),
        name="forward",
    )(send, w_gate, w_up, w_down)
    x, g, act, d1, d3 = outs[:5]
    parts = outs[5:]

    got = [
        lax.ppermute(parts[r], "tp", [(i, (i + r) % m) for i in range(m)]) for r in range(1, m)
    ]

    gb = min(256, hidden)
    full = pl.BlockSpec((rows, width), lambda j: (0, 0))
    strip = pl.BlockSpec((rows, gb), lambda j: (0, j))
    grad_gate, grad_up = pl.pallas_call(
        wide_kernel,
        out_shape=[jax.ShapeDtypeStruct(w_gate.shape, low)] * 2,
        grid=(hidden // gb,),
        in_specs=[full, strip, strip],
        out_specs=[pl.BlockSpec((1, width, gb), lambda j: (0, 0, j))] * 2,
        scratch_shapes=[pltpu.VMEM((width, rows), low)],
        compiler_params=pltpu.CompilerParams(
            dimension_semantics=("arbitrary",), vmem_limit_bytes=40 * 1024 * 1024
        ),
        cost_estimate=pl.CostEstimate(
            flops=4 * rows * width * hidden, bytes_accessed=4 * width * hidden, transcendentals=0
        ),
        name="grad_wide",
    )(x, d1, d3)
    total = pl.pallas_call(
        sum_kernel,
        out_shape=jax.ShapeDtypeStruct((n, 2, CAP, cols), low),
        in_specs=[anyw] + [vmem] * m,
        out_specs=vmem,
        name="sum_parts",
    )(grad_gate, parts[0], *got)
    grad_down = pl.pallas_call(
        down_kernel,
        out_shape=jax.ShapeDtypeStruct(w_down.shape, low),
        grid=(hidden // gb,),
        in_specs=[anyw, strip, full],
        out_specs=pl.BlockSpec((1, gb, width), lambda j: (0, j, 0)),
        compiler_params=pltpu.CompilerParams(
            dimension_semantics=("arbitrary",), vmem_limit_bytes=40 * 1024 * 1024
        ),
        cost_estimate=pl.CostEstimate(
            flops=2 * rows * width * hidden, bytes_accessed=2 * width * hidden, transcendentals=0
        ),
        name="grad_down",
    )(total, act, g)

    back = lax.all_to_all(total, "exp", split_axis=0, concat_axis=0, tiled=True)
    back = back.astype(jnp.float32).reshape(EXPERTS, group, 2, CAP, cols)
    back = jnp.sum(back, axis=1).transpose(1, 0, 2, 3).reshape(2, EXPERTS * CAP, cols)

    def combine(table, values):
        return jnp.dot(
            table, values, precision=lax.Precision.HIGHEST, preferred_element_type=jnp.float32
        ).astype(low)

    return (
        combine(weighted, back[0]),
        combine(unweighted, back[1]),
        grad_gate,
        grad_up,
        grad_down,
    )


def solution(mesh):
    in_specs = (
        P("exp", "tp"),
        P("exp", "tp"),
        P("exp", None),
        P("exp", None),
        P("exp", None, "tp"),
        P("exp", None, "tp"),
        P("exp", "tp", None),
    )
    out_specs = (
        P("exp", "tp"),
        P("exp", "tp"),
        P("exp", None, "tp"),
        P("exp", None, "tp"),
        P("exp", "tp", None),
    )
    return jax.shard_map(
        per_device, mesh=mesh, in_specs=in_specs, out_specs=out_specs, check_vma=False
    )
```

time: 173 us -> 110 us (0.64)
  the two profiles are of different devices: /device:TPU:0 before, /device:TPU:11 now
where the time goes in v1:
time: 110 us
  Pallas kernels  84 us (76%)
  starting transfers between devices  7.88 us (7%)
  local copies, waits for them, and re-layouts  6.57 us (6%)
  waiting for transfers between devices  6.01 us (5%)
  matrix products  2.77 us (3%)
  other arithmetic  2 us (2%)
    pallas_call x1, Pallas kernels, per_device(): pl.pallas_call(functools.partial(forward_kernel, n, m, group, bf, depth),...  58.6 us
    pallas_call x1, Pallas kernels, per_device(): pl.pallas_call(wide_kernel, out_shape=[jax.ShapeDtypeStruct(w_gate.shape,...  14.5 us
    pallas_call x1, Pallas kernels, per_device(): pl.pallas_call(down_kernel, out_shape=jax.ShapeDtypeStruct(w_down.shape,...  8.96 us
    unnamed x20, local copies, waits for them, and re-layouts  6.16 us
    ppermute x3, waiting for transfers between devices, per_device(): lax.ppermute(parts[r], 'tp', [(i, (i + r) % m) for i in range(m)])  6.01 us
    all_to_all x1, starting transfers between devices, per_device(): back = lax.all_to_all(total, 'exp', split_axis=0, concat_axis=0, tiled=True)  4.85 us
    ppermute x3, starting transfers between devices, per_device(): lax.ppermute(parts[r], 'tp', [(i, (i + r) % m) for i in range(m)])  3.02 us
  transfers between devices with their start and end apart: 4, of which 2 were waited for; matrix products, arithmetic and copies ran while one was open for 0% of the time, Pallas kernels for 21%

profile of v1, /device:TPU:11, one launch (start us, length us, event | category | flops | bytes accessed | tf_op | source)
XLA Modules:
  0.0 110.0 jit_solution(16387179436777074670)
XLA Ops:
  0.6 0.8 copy.24
  1.4 0.1 eq.29
  1.5 0.1 fusion.7
  1.6 0.1 reduce_window_sum.11
  1.7 0.2 select_reduce_fusion.2
  1.9 0.1 reduce_sum.43
  2.0 0.1 copy.25
  2.1 0.7 multiply_add_fusion
  2.7 0.1 copy.26
  2.8 0.8 copy.27
  3.6 0.2 select_reduce_fusion
  3.8 1.1 %fusion.3 = f32[64,2048]{1,0:T(8,128)S(1)} fusion(bf16[28,1024]{1,0:T(8,128)(2,1)} %param.8, bf16[28,1024]{1,0:T(8,128)(2,1)} %param.7, f32[28,64]{1,0:T(8,128)S(1)} %get-tuple-element.29), kind=kOutput, calls=%fused_computation.10 | convolution fusion | flops 7571200 | bytes 646144 | tf_op jit(solution)/shard_map/dot_general | solution.py:16
  4.9 0.1 fusion.2
  5.0 0.7 pad_maximum_fusion.send_ref
  5.7 58.6 %forward.1 = (bf16[64,4096]{1,0:T(8,128)(2,1)}, bf16[64,4096]{1,0:T(8,128)(2,1)}, bf16[64,2048]{1,0:T(8,128)(2,1)}, bf16[64,2048]{1,0:T(8,128)(2,1)}, bf16[64,20...) custom-call(bf16[8,16,1024]{2,1,0:T(8,128)(2,1)} %pad_maximum_fusion, ...), custom_call_target="tpu_custom_call" | custom-call | flops 6442450944 | bytes 50331648 | tf_op jit(solution)/shard_map/forward/pallas_call | solution.py:205
  64.3 0.0 copy-start.1
  64.3 0.0 copy-start.2
  64.3 0.1 collective-permute-start
  64.4 2.5 %collective-permute-start.1 = (bf16[2,64,1024]{2,1,0:T(8,128)(2,1)}, bf16[2,64,1024]{2,1,0:T(8,128)(2,1)S(1)}, u32[]{:S(2)}, u32[]{:S(2)}) collective-permute-start(bf16[2,64,1024]{2,1,0:T(8,128)(2,1)} %get-tuple-element.22), channel_id=1, source_target_pairs={{0,2},{1,3},{2,0},{3,1},{4,6},{5,7},{6,4},{7,5},{8,10},{9,11},{10,... | collective-permute-start | bytes 786440 | tf_op jit(solution)/shard_map/ppermute | solution.py:237
  66.9 0.4 collective-permute-start.2
  67.4 0.0 copy-start.3
  67.4 1.0 copy-done.3
  68.4 0.0 copy-start.4
  68.4 0.9 copy-done.4
  69.4 0.0 copy-start.5
  69.4 0.9 copy-done.5
  70.3 14.5 %grad_wide.1 = (bf16[1,4096,2048]{2,1,0:T(8,128)(2,1)}, bf16[1,4096,2048]{2,1,0:T(8,128)(2,1)}) custom-call(bf16[64,4096]{1,0:T(8,128)(2,1)S(1)} %copy-done.3, bf16[64,2048]{1,0:T(8,128)(2,1)S(1)} %copy-done.4, bf16[64,2048]{1,0:T(8,128)(2,1)S(1)} %copy-done.5), custom_call_target="tpu_custom_call" | custom-call | flops 2147483648 | bytes 33554432 | tf_op jit(solution)/shard_map/grad_wide/pallas_call | solution.py:243
  84.8 0.0 collective-permute-done.rest_1_
  84.8 0.0 copy-start.6
  84.8 1.0 collective-permute-done.1.rest_2_
  85.8 0.0 copy-start.7
  85.8 5.0 %collective-permute-done.2.rest_3_ = bf16[2,64,1024]{2,1,0:T(8,128)(2,1)S(1)} collective-permute-done((bf16[2,64,1024]{2,1,0:T(8,128)(2,1)}, bf16[2,64,1024]{2,1,0:T(8,128)(2,1)S(1)}, u32[]{:S(2)}, u32[]{:S(2)}) %collective-permute-start.2) | collective-permute-done | bytes 262176 | tf_op jit(solution)/shard_map/ppermute | solution.py:237
  90.8 0.0 copy-start.8
  90.8 0.0 copy-done.6
  90.8 0.0 copy-done.7
  90.8 0.7 copy-done.8
  91.5 2.0 %sum_parts.1._ = bf16[8,2,8,1024]{3,2,1,0:T(8,128)(2,1)} custom-call(bf16[1,4096,2048]{2,1,0:T(8,128)(2,1)} %get-tuple-element.13._, bf16[2,64,1024]{2,1,0:T(8,128)(2,1)} %get-tuple-element.20.rest_0_, bf16[2,64,1024]{2,1,0:T(8,128)(2,1)} %copy-done.6, bf16[2,64,1024]{2,1,0:T(8,128)(2,1)} %copy-done.7, bf16[2,64,1024]{2,1,0:T(8,128)(2,1)} %copy-done.8), custom_call_target="tpu_custom_call" | custom-call | tf_op jit(solution)/shard_map/sum_parts/pallas_call | solution.py:258
  93.5 4.9 %all-to-all-start = ((bf16[8,2,8,1024]{3,2,1,0:T(8,128)(2,1)}), bf16[8,2,8,1024]{3,2,1,0:T(8,128)(2,1)S(1)}, u32[]{:S(2)}, u32[]{:S(2)}) async-start(bf16[8,2,8,1024]{3,2,1,0:T(8,128)(2,1)} %sum_parts.1._), calls=%async_computation | async-start | bytes 524288 | tf_op jit(solution)/shard_map/all_to_all | solution.py:280
  98.4 0.0 copy-done.1
  98.4 0.0 copy-done.2
  98.4 0.0 copy-start
  98.4 1.0 copy-done
  99.4 9.0 %grad_down.1 = bf16[1,2048,4096]{2,1,0:T(8,128)(2,1)} custom-call(bf16[8,2,8,1024]{3,2,1,0:T(8,128)(2,1)S(1)} %copy-done, bf16[64,2048]{1,0:T(8,128)(2,1)S(1)} %copy-done.2, bf16[64,4096]{1,0:T(8,128)(2,1)S(1)} %copy-done.1), custom_call_target="tpu_custom_call" | custom-call | flops 1073741824 | bytes 16777216 | tf_op jit(solution)/shard_map/grad_down/pallas_call | solution.py:265
  108.3 0.0 all-to-all-done
  108.3 0.8 convolution_convert_fusion
  109.2 0.8 convolution_convert_fusion.1
  (1 shorter events, 0.0 us)
Async XLA Ops:
  64.3 34.1 %copy-start.1 = (bf16[64,4096]{1,0:T(8,128)(2,1)S(1)}, bf16[64,4096]{1,0:T(8,128)(2,1)}, u32[]{:S(2)}) copy-start(bf16[64,4096]{1,0:T(8,128)(2,1)} %get-tuple-element.26.g_ref) | copy-start | bytes 1572868
  64.3 34.1 %copy-start.2 = (bf16[64,2048]{1,0:T(8,128)(2,1)S(1)}, bf16[64,2048]{1,0:T(8,128)(2,1)}, u32[]{:S(2)}) copy-start(bf16[64,2048]{1,0:T(8,128)(2,1)} %get-tuple-element.25.a_ref) | copy-start | bytes 786436
  64.3 20.5 %collective-permute-start = (bf16[2,64,1024]{2,1,0:T(8,128)(2,1)}, bf16[2,64,1024]{2,1,0:T(8,128)(2,1)S(1)}, u32[]{:S(2)}, u32[]{:S(2)}) collective-permute-start(bf16[2,64,1024]{2,1,0:T(8,128)(2,1)} %get-tuple-element.21), channel_id=1, source_target_pairs={{0,1},{1,2},{2,3},{3,0},{4,5},{5,6},{6,7},{7,4},{8,9},{9,10},{10,1... | collective-permute-start | bytes 786440 | tf_op jit(solution)/shard_map/ppermute | solution.py:237
  64.4 21.4 %collective-permute-start.1 = (bf16[2,64,1024]{2,1,0:T(8,128)(2,1)}, bf16[2,64,1024]{2,1,0:T(8,128)(2,1)S(1)}, u32[]{:S(2)}, u32[]{:S(2)}) collective-permute-start(bf16[2,64,1024]{2,1,0:T(8,128)(2,1)} %get-tuple-element.22), channel_id=1, source_target_pairs={{0,2},{1,3},{2,0},{3,1},{4,6},{5,7},{6,4},{7,5},{8,10},{9,11},{10,... | collective-permute-start | bytes 786440 | tf_op jit(solution)/shard_map/ppermute | solution.py:237
  66.9 23.9 %collective-permute-start.2 = (bf16[2,64,1024]{2,1,0:T(8,128)(2,1)}, bf16[2,64,1024]{2,1,0:T(8,128)(2,1)S(1)}, u32[]{:S(2)}, u32[]{:S(2)}) collective-permute-start(bf16[2,64,1024]{2,1,0:T(8,128)(2,1)} %get-tuple-element.23), channel_id=1, source_target_pairs={{0,3},{1,0},{2,1},{3,2},{4,7},{5,4},{6,5},{7,6},{8,11},{9,8},{10,9... | collective-permute-start | bytes 786440 | tf_op jit(solution)/shard_map/ppermute | solution.py:237
  67.4 1.0 copy-start.3
  68.4 0.9 copy-start.4
  69.4 0.9 copy-start.5
  84.8 6.0 %copy-start.6 = (bf16[2,64,1024]{2,1,0:T(8,128)(2,1)}, bf16[2,64,1024]{2,1,0:T(8,128)(2,1)S(1)}, u32[]{:S(2)}) copy-start(bf16[2,64,1024]{2,1,0:T(8,128)(2,1)S(1)} %collective-permute-done.rest_1_) | copy-start | bytes 786436
  85.8 5.0 %copy-start.7 = (bf16[2,64,1024]{2,1,0:T(8,128)(2,1)}, bf16[2,64,1024]{2,1,0:T(8,128)(2,1)S(1)}, u32[]{:S(2)}) copy-start(bf16[2,64,1024]{2,1,0:T(8,128)(2,1)S(1)} %collective-permute-done.1.rest_2_) | copy-start | bytes 786436
  90.8 0.7 copy-start.8
  93.5 14.8 %all-to-all-start = ((bf16[8,2,8,1024]{3,2,1,0:T(8,128)(2,1)}), bf16[8,2,8,1024]{3,2,1,0:T(8,128)(2,1)S(1)}, u32[]{:S(2)}, u32[]{:S(2)}) async-start(bf16[8,2,8,1024]{3,2,1,0:T(8,128)(2,1)} %sum_parts.1._), calls=%async_computation | async-start | bytes 524288 | tf_op jit(solution)/shard_map/all_to_all | solution.py:280
  98.4 1.0 copy-start
